TPU v7x, 32 devices: a 4x4x1 block of a 4x4x8 slice. The times are simulated.
32 devices in a mesh: data: 1 (over z), model: 32 (over y, x, core).
Axes of the slice: x: 4, y: 4, z: 1, core: 2. Of those that a mesh axis runs over, the one named last changes fastest.
The devices are a block of a 4x4x8 slice.
Arguments:
- queries: bfloat16 [32, 896], P('data')
- w_head: bfloat16 [896, 151936], P(None, 'model')
- ds_keys: bfloat16 [524288, 896], P('model')
- ds_tokens: int32 [524288], P('model')
- temperature: float32 [1], replicated
- mix_weight: float32 [1], replicated
Outputs:
- output: float32 [32, 151936], P('data', 'model')
All inputs are finite; a program needn't handle non-finite values.
Results may differ from a plain program's by a relative error of at most 0.001.
Values are sent between devices in bfloat16 or wider.
A program may use at most 768 MiB of HBM per device.

v0:
```python
import jax
import jax.numpy as jnp
from jax import lax
from jax.sharding import PartitionSpec as P


def solution(mesh):
    group_size = mesh.shape["model"]

    def local_step(queries, w_shard, key_shard, tok_shard, value_a11, mix_weight):
        row_count = queries.shape[0]
        vocab_size = w_shard.shape[1] * group_size
        cross_dot = jnp.einsum("bd,nd->bn", queries, key_shard, preferred_element_type=jnp.float32)
        key_sq = jnp.sum(jnp.square(key_shard.astype(jnp.float32)), axis=1)
        scores = (2.0 * cross_dot - key_sq[None, :]) / value_a11[0]
        row_max = lax.pmax(jnp.max(scores, axis=1), "model")
        weights = jnp.exp(scores - row_max[:, None])
        row_total = lax.psum(jnp.sum(weights, axis=1), "model")
        local_hist = jnp.zeros((row_count, vocab_size), jnp.float32).at[:, tok_shard].add(weights)
        histogram = lax.psum_scatter(local_hist, "model", scatter_dimension=1, tiled=True)
        logits = jnp.dot(queries, w_shard, preferred_element_type=jnp.float32)
        lm_max = lax.pmax(jnp.max(logits, axis=1), "model")
        lm_exp = jnp.exp(logits - lm_max[:, None])
        lm_total = lax.psum(jnp.sum(lm_exp, axis=1), "model")
        mix_value = mix_weight[0]
        p_knn = histogram / row_total[:, None]
        p_lm = lm_exp / lm_total[:, None]
        return jnp.log(mix_value * p_knn + (1.0 - mix_value) * p_lm)

    return jax.shard_map(
        local_step,
        mesh=mesh,
        in_specs=(P("data", None), P(None, "model"), P("model", None), P("model"), P(), P()),
        out_specs=P("data", "model"),
        check_vma=False,
    )
```

profile of v0, /device:TPU:97, one launch (start us, length us, event | category | flops | bytes accessed | tf_op | source)
XLA Modules:
  0.0 550.7 jit_solution(9816768189804503707)
XLA Ops:
  6.5 0.0 copy-start
  6.6 0.0 all-reduce.5.cloned.1.call-start
  6.6 0.9 compare_select_fusion
  8.1 18.0 %multiply_reduce_fusion = f32[16384]{0:T(1024)S(1)} fusion(bf16[16384,896]{1,0:T(8,128)(2,1)} %param.8), kind=kLoop, calls=%fused_computation.2 | loop fusion | flops 44023808 | bytes 29425664 | tf_op jit(solution)/shard_map/reduce_sum | solution.py:14
  26.1 0.0 copy-done
  26.1 6.0 %fusion.15 = (f32[32]{0:T(128)S(1)}, f32[32,4748]{1,0:T(8,128)S(1)}) fusion(bf16[32,896]{1,0:T(8,128)(2,1)S(1)} %copy-done, bf16[896,4748]{0,1:T(8,128)(2,1)} %param.7), kind=kOutput, calls=%fused_computation.21 | convolution fusion | flops 272421216 | bytes 9173632 | tf_op jit(solution)/shard_map/dot_general | solution.py:21
  32.1 15.2 %fusion.14 = (f32[32]{0:T(128)S(1)}, f32[32,16384]{1,0:T(8,128)}) fusion(f32[]{:T(128)} %bitcast.10, f32[16384]{0:T(1024)S(1)} %multiply_reduce_fusion, bf16[32,896]{1,0:T(8,128)(2,1)S(1)} %copy-done, bf16[16384,896]{1,0:T(8,128)(2,1)} %param.8), kind=kOutput, calls=%fused_computation.20 | convolution fusion | flops 941621248 | bytes 31580292 | tf_op jit(solution)/shard_map/bd,nd->bn/dot_general | solution.py:13
  47.3 50.0 %all-reduce.2 = (f32[32]{0:T(128)S(1)}, f32[32]{0:T(128)S(1)}) all-reduce(f32[32]{0:T(128)S(1)} %get-tuple-element.13, f32[32]{0:T(128)S(1)} %get-tuple-element.15), channel_id=1, replica_groups=mesh['data'=1,'model'=32] {'model'}, use_global_device_ids=true, to_apply=%region_2.0 | all-reduce | flops 64 | bytes 512 | tf_op jit(solution)/shard_map/pmax | solution.py:16
  97.3 2.0 fusion.8
  99.3 4.8 copy.9
  104.1 7.1 %sort = (s32[16384]{0:T(1024)S(1)}, s32[16384]{0:T(1024)S(1)}) sort(s32[16384]{0:T(1024)S(1)} %compare_select_fusion, s32[16384]{0:T(1024)S(1)} %iota), dimensions={0}, to_apply=%compare | sort | flops 229376 | bytes 262144 | tf_op jit(solution)/shard_map/scatter-add | solution.py:19
  111.3 212.5 %scatter_custom_fusion = f32[32,151936]{0,1:T(8,128)} fusion(s32[16384]{0:T(1024)S(1)} %get-tuple-element.5, f32[]{:T(128)} %constant.6.clone.1, f32[16384,32]{1,0:T(8,128)} %copy.9, s32[16384]{0:T(1024)S(1)} %broadcast_clamp_fusion), kind=kCustom, calls=%fused_computation.3 | custom fusion | flops 524288 | bytes 19448320 | tf_op jit(solution)/shard_map/scatter-add | solution.py:19
  323.8 46.7 %copy.10 = f32[32,151936]{1,0:T(8,128)} copy(f32[32,151936]{0,1:T(8,128)} %scatter_custom_fusion) | data formatting | bytes 38895616 | tf_op jit(solution)/shard_map/scatter-add | solution.py:19
  370.6 0.0 copy-start.1
  370.6 0.1 all-reduce.5.cloned.1.call-update
  371.3 0.3 fusion.13
  371.6 44.9 %all-reduce.1 = (f32[32]{0:T(128)S(1)}, f32[32]{0:T(128)S(1)}) all-reduce(f32[32]{0:T(128)S(1)} %fusion.13, f32[32]{0:T(128)S(1)} %get-tuple-element.11), channel_id=1, replica_groups=mesh['data'=1,'model'=32] {'model'}, use_global_device_ids=true, to_apply=%region_10.0 | all-reduce | flops 64 | bytes 512 | tf_op jit(solution)/shard_map/psum | solution.py:24
  416.4 125.2 %all-reduce.5.cloned.1.call-done = f32[32,151936]{1,0:T(8,128)} async-done(((f32[32,151936]{1,0:T(8,128)}), f32[32,151936]{1,0:T(8,128)}) %all-reduce.5.cloned.1.call-update) | async-done | bytes 19447824
  541.6 2.2 fusion.12
  543.8 0.0 copy-done.1
  (2 shorter events, 0.0 us)
Async XLA Ops:
  6.5 19.5 %copy-start = (bf16[32,896]{1,0:T(8,128)(2,1)S(1)}, bf16[32,896]{1,0:T(8,128)(2,1)}, u32[]{:S(2)}) copy-start(bf16[32,896]{1,0:T(8,128)(2,1)} %param.6) | copy-start | bytes 172036
  6.6 535.1 %all-reduce.5.cloned.1.call-start = ((), (), s32[]{:S(2)}) async-start(), calls=%async_computation | async-start | bytes 38895616
  370.6 173.3 %copy-start.1 = (bf16[32,896]{1,0:T(8,128)(2,1)S(1)}, bf16[32,896]{1,0:T(8,128)(2,1)}, u32[]{:S(2)}) copy-start(bf16[32,896]{1,0:T(8,128)(2,1)} %param.6) | copy-start | bytes 172036
Sparse Core Ops, SparseCore 0:
  370.7 170.8 all-reduce.4
where the time goes:
time: 553 us; the launch traced here: 551 us
  other arithmetic  243 us (44%)
  waiting for transfers between devices  125 us (23%)
  blocking collectives  94.9 us (17%)
  local copies, waits for them, and re-layouts  51.5 us (9%)
  matrix products  21.2 us (4%)
  between operations  14.8 us (3%)
    scatter-add x3, other arithmetic, local_step(): jnp.zeros((row_count, vocab_size), jnp.float32).at[:, tok_shard]  220 us
    unnamed x2, waiting for transfers between devices  125 us
    pmax x1, blocking collectives, local_step(): row_max = lax.pmax(jnp.max(scores, axis=1), 'model')  50 us
    scatter-add x2, local copies, waits for them, and re-layouts, local_step(): jnp.zeros((row_count, vocab_size), jnp.float32).at[:, tok_shard]  46.7 us
    psum x1, blocking collectives, local_step(): lm_total = lax.psum(jnp.sum(lm_exp, axis=1), 'model')  44.9 us
    reduce_sum x1, other arithmetic, local_step(): key_sq = jnp.sum(jnp.square(key_shard.astype(jnp.float32)), axis=1)  18 us
    dot_general x1, matrix products, local_step(): jnp.einsum('bd,nd->bn', queries, key_shard, preferred_element_type=jnp.fl...  15.2 us
  transfers between devices with their start and end apart: 1, of which 1 were waited for; matrix products, arithmetic and copies ran while one was open for 0% of the time, Pallas kernels for 0%

commit v1 on v0

v1 whole, which is shorter than its diff:
```python
import functools

import jax
import jax.numpy as jnp
from jax import lax
from jax.experimental import pallas as pl
from jax.experimental.pallas import tpu as pltpu
from jax.sharding import PartitionSpec as P

MESH = pl.DeviceIdType.MESH
LANES = 128
BLK = 1024
SUB = 256
F32 = jnp.float32


def _bit_reverse(k, bits):
    out = 0
    for i in range(bits):
        out |= ((k >> i) & 1) << (bits - 1 - i)
    return out


def _exchange_kernel(
    cfg, start_ref, inv_ref, tau_ref, q4_ref, q_ref, tok_ref, keys_hbm, w_hbm,
    recv_ref, stats_out, logits_ref,
    kbuf, scores, wbuf, send, stats, stats_recv,
    ksem, wsem, lsem, send_sem, recv_sem, ssend_sem, srecv_sem, osem,
):
    group, rows, cap, cols, copies, vrows = cfg
    me = lax.axis_index("model")
    n_local = keys_hbm.shape[0]
    nblk = n_local // BLK
    crows = cap // copies
    qrows = q_ref.shape[0]

    barrier = pltpu.get_barrier_semaphore()

    @pl.loop(1, group)
    def _(k):
        peer = lax.rem(me + k, group)
        pl.semaphore_signal(barrier, inc=1, device_id={"model": peer}, device_id_type=MESH)

    def key_copy(b, slot):
        return pltpu.make_async_copy(keys_hbm.at[pl.ds(b * BLK, BLK), :], kbuf.at[slot], ksem.at[slot])

    key_copy(0, 0).start()
    key_copy(1, 1).start()
    w_copy = pltpu.make_async_copy(w_hbm, wbuf, wsem)
    tau = tau_ref[0]

    def block(b, best):
        slot = lax.rem(b, 3)

        @pl.when(b + 2 < nblk)
        def _():
            key_copy(b + 2, lax.rem(b + 2, 3)).start()

        key_copy(b, slot).wait()

        def piece(p, best):
            x = kbuf[slot, pl.ds(p * SUB, SUB), :]
            dot = jnp.dot(x, q4_ref[...], preferred_element_type=F32)
            xf = x.astype(F32)
            sq = jnp.square(xf[:, :LANES])
            for j in range(1, x.shape[1] // LANES):
                sq = sq + jnp.square(xf[:, j * LANES:(j + 1) * LANES])
            norm = jnp.sum(sq, axis=1, keepdims=True)
            s = (2.0 * dot - norm) / tau
            scores[pl.ds(b * BLK + p * SUB, SUB), :] = s
            return jnp.maximum(best, jnp.max(s.reshape(SUB // 8, 8, LANES), axis=0))

        return lax.fori_loop(0, BLK // SUB, piece, best)

    best = lax.fori_loop(0, nblk, block, jnp.full((8, LANES), -jnp.inf, F32))
    w_copy.start()
    row_max = jnp.max(best, axis=0, keepdims=True)

    pl.semaphore_wait(barrier, group - 1)

    lane_group = lax.broadcasted_iota(jnp.int32, (1, LANES), 1) // qrows
    entry = (
        lax.broadcasted_iota(jnp.int32, (crows, LANES), 0) * copies
        + lax.broadcasted_iota(jnp.int32, (crows, LANES), 1) // qrows
    )
    id_pos = lax.broadcasted_iota(jnp.int32, (8, LANES), 0) * LANES + lax.broadcasted_iota(jnp.int32, (8, LANES), 1)
    id_lane = lax.broadcasted_iota(jnp.int32, (8, LANES), 1)

    def block_send(k, dest):
        return pltpu.make_async_remote_copy(
            src_ref=send.at[k], dst_ref=recv_ref.at[me], send_sem=send_sem.at[k], recv_sem=recv_sem.at[me],
            device_id={"model": dest}, device_id_type=MESH,
        )

    bits = group.bit_length() - 1

    def offset_of(j):
        k = 0
        for i in range(bits):
            k = k + lax.rem(lax.div(j, 1 << i), 2) * (1 << (bits - 1 - i))
        return k

    def pack(k, total):
        dest = lax.rem(me + k, group)
        first = start_ref[dest]
        count = start_ref[dest + 1] - first

        @pl.loop(0, crows // 8)
        def _(t):
            base = first + t * (8 * copies)
            for r in range(8):
                parts = [scores[pl.ds(inv_ref[base + r * copies + g], 1), :] for g in range(copies)]
                row = parts[copies - 1]
                for g in range(copies - 2, -1, -1):
                    row = jnp.where(lane_group == g, parts[g], row)
                send[k, pl.ds(t * 8 + r, 1), :] = row

        w = jnp.where(entry < count, jnp.exp(send[k, :crows, :] - row_max), 0.0)
        send[k, :crows, :] = w
        shift = lax.rem(first, LANES)
        at = lax.div(first, LANES)
        low = pltpu.roll(tok_ref[pl.ds(at, 8), :], LANES - shift, axis=1)
        high = pltpu.roll(tok_ref[pl.ds(at + 1, 8), :], LANES - shift, axis=1)
        tok = jnp.where(id_lane < LANES - shift, low, high) - dest * cols
        send[k, crows:crows + 8, :] = jnp.where(id_pos < count, tok, cols).astype(F32)
        return total + jnp.sum(w.reshape(crows // 8, 8, LANES), axis=0)

    def step(j, total):
        k = offset_of(j)
        total = pack(k, total)
        block_send(k, lax.rem(me + k, group)).start()
        return total

    total = lax.fori_loop(1, group, step, jnp.zeros((8, LANES), F32))
    total = pack(0, total)
    own = pltpu.make_async_copy(send.at[0], recv_ref.at[me], lsem)
    own.start()

    w_copy.wait()
    def head(at, size, carry):
        lm_max, lm_sum = carry
        x = jnp.dot(wbuf[pl.ds(at, size), :], q4_ref[...], preferred_element_type=F32)
        logits_ref[pl.ds(at, size), :] = x
        new = jnp.maximum(lm_max, jnp.max(x, axis=0, keepdims=True))
        return new, lm_sum * jnp.exp(lm_max - new) + jnp.sum(jnp.exp(x - new), axis=0, keepdims=True)

    carry = (jnp.full((1, LANES), -jnp.inf, F32), jnp.zeros((1, LANES), F32))
    carry = lax.fori_loop(0, cols // SUB, lambda i, c: head(i * SUB, SUB, c), carry)
    if cols % SUB:
        carry = head(cols // SUB * SUB, cols % SUB, carry)
    lm_max_row, lm_sum_row = carry

    def worst(d, c):
        return jnp.maximum(c, start_ref[d + 1] - start_ref[d])

    most = lax.fori_loop(0, group, worst, jnp.int32(0))
    over = jnp.where(most > cap, 1.0, 0.0).astype(F32)
    stats[0:1, :] = row_max
    stats[1:2, :] = jnp.sum(total, axis=0, keepdims=True)
    stats[2:3, :] = lm_max_row
    stats[3:4, :] = lm_sum_row
    stats[4:5, :] = jnp.full((1, LANES), over, F32)
    stats[5:8, :] = jnp.zeros((3, LANES), F32)

    def stat_send(k, dest):
        return pltpu.make_async_remote_copy(
            src_ref=stats, dst_ref=stats_recv.at[me], send_sem=ssend_sem.at[k], recv_sem=srecv_sem.at[me],
            device_id={"model": dest}, device_id_type=MESH,
        )

    @pl.loop(1, group)
    def _(k):
        stat_send(k, lax.rem(me + k, group)).start()

    stats_recv[me] = stats[...]

    @pl.loop(1, group)
    def _(k):
        src = lax.rem(me + group - k, group)
        pltpu.make_async_remote_copy(
            src_ref=stats, dst_ref=stats_recv.at[src], send_sem=ssend_sem.at[k], recv_sem=srecv_sem.at[src],
            device_id={"model": src}, device_id_type=MESH,
        ).wait_recv()
        pltpu.make_async_remote_copy(
            src_ref=send.at[k], dst_ref=recv_ref.at[src], send_sem=send_sem.at[k], recv_sem=recv_sem.at[src],
            device_id={"model": src}, device_id_type=MESH,
        ).wait_recv()

    @pl.loop(1, group)
    def _(k):
        block_send(k, lax.rem(me + k, group)).wait_send()
        stat_send(k, lax.rem(me + k, group)).wait_send()

    own.wait()
    stats_out[...] = stats_recv[...]


def _finish_kernel(
    cfg, mix_ref, stats_ref, recv_ref, logits_ref, out_ref, hist0, hist1, hist2, hist3, scaled, idbuf, ids, sem
):
    group, rows, cap, cols, copies, vrows = cfg
    crows = cap // copies
    hists = (hist0, hist1, hist2, hist3)
    idbuf[...] = recv_ref[:, crows:crows + 8, :].astype(jnp.int32)
    id_copy = pltpu.make_async_copy(idbuf, ids, sem)
    id_copy.start()

    st = stats_ref[...]
    m_all = st[:, 0, :]
    m = jnp.max(m_all, axis=0, keepdims=True)
    scale = jnp.exp(m_all - m)
    z = jnp.sum(st[:, 1, :] * scale, axis=0, keepdims=True)
    lm_all = st[:, 2, :]
    lm = jnp.max(lm_all, axis=0, keepdims=True)
    lmz = jnp.sum(st[:, 3, :] * jnp.exp(lm_all - lm), axis=0, keepdims=True)

    @pl.loop(0, vrows // 8)
    def _(i):
        for h in hists:
            h[pl.ds(i * 8, 8), :] = jnp.zeros((8, LANES), F32)

    for s in range(group):
        scaled[s] = recv_ref[s, :crows, :] * scale[s:s + 1, :]
    id_copy.wait()

    @pl.loop(0, group)
    def _(s):
        @pl.loop(0, crows // 8)
        def _(t):
            sub = lax.div(t, LANES // (8 * copies))
            lane0 = lax.rem(t, LANES // (8 * copies)) * (8 * copies)
            for r in range(8):
                row = scaled[s, pl.ds(t * 8 + r, 1), :]
                for g in range(copies):
                    v = ids[s, sub, lane0 + r * copies + g]
                    hists[g][pl.ds(v, 1), :] = hists[g][pl.ds(v, 1), :] + row

    qrows = out_ref.shape[0]
    lane = lax.broadcasted_iota(jnp.int32, (LANES, LANES), 1)
    eye = lane == lax.broadcasted_iota(jnp.int32, (LANES, LANES), 0)

    def column(row):
        return jnp.sum(jnp.where(eye, row, 0.0), axis=1, keepdims=True)

    zc = column(z)
    z_col = zc[:qrows]
    for g in range(1, copies):
        z_col = z_col + zc[g * qrows:(g + 1) * qrows]
    lmz_col = column(lmz)[:qrows]
    mix = mix_ref[0]
    a = mix / z_col
    b = (1.0 - mix) / lmz_col
    for c in range(pl.cdiv(cols, LANES)):
        width = min(LANES, cols - c * LANES)
        hrows = min(LANES, vrows - c * LANES)
        acc = hists[0][c * LANES:c * LANES + hrows, :]
        for g in range(1, copies):
            acc = jnp.where(lane[:hrows] // qrows >= g, hists[g][c * LANES:c * LANES + hrows, :], acc)
        if hrows < LANES:
            acc = jnp.concatenate([acc, jnp.zeros((LANES - hrows, LANES), F32)], axis=0)
        tr = acc.T
        h = tr[:qrows]
        for g in range(1, copies):
            h = h + tr[g * qrows:(g + 1) * qrows]
        e = jnp.exp(logits_ref[c * LANES:c * LANES + width, :] - lm)
        if width < LANES:
            e = jnp.concatenate([e, jnp.zeros((LANES - width, LANES), F32)], axis=0)
        e = e.T[:qrows, :width]
        out_ref[:, c * LANES:c * LANES + width] = jnp.log(h[:, :width] * a + e * b)


def solution(mesh):
    group = mesh.shape["model"]

    def dense_path(queries, w_shard, key_shard, tok_shard, temperature, mix_weight):
        row_count = queries.shape[0]
        cols = w_shard.shape[1]
        cross_dot = jnp.einsum("bd,nd->bn", queries, key_shard, preferred_element_type=F32)
        key_sq = jnp.sum(jnp.square(key_shard.astype(F32)), axis=1)
        scores = (2.0 * cross_dot - key_sq[None, :]) / temperature[0]
        row_max = lax.pmax(jnp.max(scores, axis=1), "model")
        weights = jnp.exp(scores - row_max[:, None])
        row_total = lax.psum(jnp.sum(weights, axis=1), "model")
        local_hist = jnp.zeros((row_count, cols * group), F32).at[:, tok_shard].add(weights)
        pieces = jnp.transpose(local_hist.reshape(row_count, group, cols), (1, 0, 2))
        histogram = jnp.sum(lax.all_to_all(pieces, "model", 0, 0), axis=0)
        logits = jnp.dot(queries, w_shard, preferred_element_type=F32)
        lm_max = lax.pmax(jnp.max(logits, axis=1), "model")
        lm_exp = jnp.exp(logits - lm_max[:, None])
        lm_total = lax.psum(jnp.sum(lm_exp, axis=1), "model")
        mix = mix_weight[0]
        return jnp.log(mix * (histogram / row_total[:, None]) + (1.0 - mix) * (lm_exp / lm_total[:, None]))

    def local_step(queries, w_shard, key_shard, tok_shard, temperature, mix_weight):
        rows, dim = queries.shape
        n_local = key_shard.shape[0]
        cols = w_shard.shape[1]
        copies = LANES // rows
        mean = n_local // group
        cap = -(-int(mean + 5.6 * mean ** 0.5) // 32) * 32
        crows = cap // copies
        vrows = (cols // 8 + 1) * 8
        cfg = (group, rows, cap, cols, copies, vrows)

        tok_sorted, inv = lax.sort((tok_shard, lax.iota(jnp.int32, n_local)), num_keys=1)
        bounds = lax.iota(jnp.int32, group + 1) * cols
        start = jnp.sum((tok_sorted[None, :] < bounds[:, None]).astype(jnp.int32), axis=1)
        inv = jnp.pad(inv, (0, cap))
        tok2d = jnp.pad(tok_sorted, (0, 16 * LANES)).reshape(n_local // LANES + 16, LANES)
        q4 = jnp.tile(queries.T, (1, copies))

        smem = pl.BlockSpec(memory_space=pltpu.SMEM)
        vmem = pl.BlockSpec(memory_space=pltpu.VMEM)
        hbm = pl.BlockSpec(memory_space=pl.ANY)
        recv, stats, logits = pl.pallas_call(
            functools.partial(_exchange_kernel, cfg),
            out_shape=(
                jax.ShapeDtypeStruct((group, crows + 8, LANES), F32),
                jax.ShapeDtypeStruct((group, 8, LANES), F32),
                jax.ShapeDtypeStruct((cols, LANES), F32),
            ),
            in_specs=[smem, smem, smem, vmem, vmem, vmem, hbm, hbm],
            out_specs=(hbm, vmem, vmem),
            scratch_shapes=[
                pltpu.VMEM((3, BLK, dim), jnp.bfloat16),
                pltpu.VMEM((n_local, LANES), F32),
                pltpu.VMEM((cols, dim), jnp.bfloat16),
                pltpu.VMEM((group, crows + 8, LANES), F32),
                pltpu.VMEM((8, LANES), F32),
                pltpu.VMEM((group, 8, LANES), F32),
                pltpu.SemaphoreType.DMA((3,)),
                pltpu.SemaphoreType.DMA,
                pltpu.SemaphoreType.DMA,
                pltpu.SemaphoreType.DMA((group,)),
                pltpu.SemaphoreType.DMA((group,)),
                pltpu.SemaphoreType.DMA((group,)),
                pltpu.SemaphoreType.DMA((group,)),
                pltpu.SemaphoreType.DMA,
            ],
            compiler_params=pltpu.CompilerParams(
                collective_id=0, has_side_effects=True, vmem_limit_bytes=60 * 1024 * 1024
            ),
            name="knn_exchange",
        )(start, inv, temperature, q4, queries, tok2d, key_shard, w_shard.T)

        fast = pl.pallas_call(
            functools.partial(_finish_kernel, cfg),
            out_shape=jax.ShapeDtypeStruct((rows, cols), F32),
            in_specs=[smem, vmem, vmem, vmem],
            out_specs=vmem,
            scratch_shapes=[pltpu.VMEM((vrows, LANES), F32)] * 4
            + [
                pltpu.VMEM((group, crows, LANES), F32),
                pltpu.VMEM((group, 8, LANES), jnp.int32),
                pltpu.SMEM((group, 8, LANES), jnp.int32),
                pltpu.SemaphoreType.DMA,
            ],
            compiler_params=pltpu.CompilerParams(vmem_limit_bytes=60 * 1024 * 1024),
            name="knn_finish",
        )(mix_weight, stats, recv, logits)

        overflow = jnp.max(stats[:, 4, 0]) > 0.0
        args = (queries, w_shard, key_shard, tok_shard, temperature, mix_weight)
        return lax.cond(overflow, lambda: dense_path(*args), lambda: fast)

    return jax.shard_map(
        local_step,
        mesh=mesh,
        in_specs=(P("data", None), P(None, "model"), P("model", None), P("model"), P(), P()),
        out_specs=P("data", "model"),
        check_vma=False,
    )
```

time: 553 us -> 152 us (0.27)
  other arithmetic: 243 us -> 10.6 us
  Pallas kernels: 0 us -> 135 us
  waiting for transfers between devices: 125 us -> 0 us
  blocking collectives: 94.9 us -> 0 us
  local copies, waits for them, and re-layouts: 51.5 us -> 3.78 us
  matrix products: 21.2 us -> 0 us
  between operations: 14.8 us -> 2.02 us
    scatter-add x3 -> x0, other arithmetic: 220 us -> none  [local_step(): jnp.zeros((row_count, vocab_size), jnp.float32).at[:, tok_shard]]
    pallas_call x0 -> x2, Pallas kernels: none -> 135 us  [the longest x1 72.4 us: local_step(): pl.pallas_call(functools.partial(_exchange_kernel, cfg), out_shape=(jax.S...]
    unnamed x2 -> x0, waiting for transfers between devices: 125 us -> none
    pmax x1 -> x0, blocking collectives: 50 us -> none  [local_step(): row_max = lax.pmax(jnp.max(scores, axis=1), 'model')]
    scatter-add x2 -> x0, local copies, waits for them, and re-layouts: 46.7 us -> none  [local_step(): jnp.zeros((row_count, vocab_size), jnp.float32).at[:, tok_shard]]
    psum x1 -> x0, blocking collectives: 44.9 us -> none  [local_step(): lm_total = lax.psum(jnp.sum(lm_exp, axis=1), 'model')]
    dot_general x2 -> x0, matrix products: 21.2 us -> none  [the longest x1 15.2 us: local_step(): jnp.einsum('bd,nd->bn', queries, key_shard, preferred_element_type=jnp.fl...]
    reduce_sum x3 -> x1, other arithmetic: 20.3 us -> 1.06 us  [local_step(): jnp.sum((tok_sorted[None, :] < bounds[:, None]).astype(jnp.int32), axis=1)]
  transfers between devices with their start and end apart: 1 -> 0, of which waited for: 1 -> 0; matrix products, arithmetic and copies ran while one was open for 0% -> 0% of each run, Pallas kernels for 0% -> 0%
where the time goes in v1:
time: 152 us
  Pallas kernels  135 us (89%)
  other arithmetic  10.6 us (7%)
  local copies, waits for them, and re-layouts  3.78 us (2%)
  between operations  2.02 us (1%)
    pallas_call x1, Pallas kernels, local_step(): pl.pallas_call(functools.partial(_exchange_kernel, cfg), out_shape=(jax.S...  72.4 us
    pallas_call x1, Pallas kernels, local_step(): pl.pallas_call(functools.partial(_finish_kernel, cfg), out_shape=jax.Shap...  62.6 us
    sort x1, other arithmetic, local_step(): lax.sort((tok_shard, lax.iota(jnp.int32, n_local)), num_keys=1)  7.97 us

profile of v1, /device:TPU:97, one launch (start us, length us, event | category | flops | bytes accessed | tf_op | source)
XLA Modules:
  0.0 151.6 jit_solution(935726526023509113)
XLA Ops:
  0.0 8.0 %sort.15 = (s32[16384]{0:T(1024)S(1)}, s32[16384]{0:T(1024)S(1)}) sort(s32[16384]{0:T(1024)} %param.11, s32[16384]{0:T(1024)S(1)} %iota.8), dimensions={0}, to_apply=%region_0.0 | sort | flops 229376 | bytes 262144 | tf_op jit(solution)/shard_map/sort | solution.py:305
  8.0 1.1 convert_reduce_fusion.start_ref
  9.1 0.6 pad.8.inv_ref
  10.3 0.8 tile.4
  11.2 0.8 copy.24.q4_ref
  12.0 0.6 pad_bitcast_fusion.tok_ref
  12.6 0.0 copy-start
  12.7 0.0 copy-start.2
  12.7 72.4 %knn_exchange.1 = (f32[32,168,128]{2,1,0:T(8,128)}, f32[32,8,128]{2,1,0:T(8,128)}, f32[4748,128]{1,0:T(8,128)}) custom-call(s32[33]{0:T(128)} %convert_reduce_fusion.start_ref, s32[17024]{0:T(1024)} %pad.8.inv_ref, f32[1]{0:T(128)S(6)} %copy.29.tau_ref, bf16[896,128]{1,0:T(8,128)(2,1)} %copy.24.q4_ref, bf16[32,896]{1,0:T(8,128)(2,1)} %q_ref.1, ...), custom_call_target="tpu_custom_call" | custom-call | tf_op jit(solution)/shard_map/knn_exchange/pallas_call | solution.py:315
  85.0 1.5 %slice_reduce_fusion = f32[]{:T(128)} fusion(f32[32,8,128]{2,1,0:T(8,128)} %get-tuple-element.34.stats_ref), kind=kLoop, calls=%fused_computation.19 | loop fusion | flops 31 | bytes 132 | tf_op jit(solution)/shard_map/reduce_max | solution.py:362
  87.9 62.6 %knn_finish.1 = f32[32,4748]{1,0:T(8,128)S(1)} custom-call(f32[1]{0:T(128)S(6)} %copy.30.mix_ref, f32[32,8,128]{2,1,0:T(8,128)} %get-tuple-element.34.stats_ref, f32[32,168,128]{2,1,0:T(8,128)} %get-tuple-element.35.recv_ref, f32[4748,128]{1,0:T(8,128)} %get-tuple-element.36.logits_ref), custom_call_target="tpu_custom_call" | custom-call | tf_op jit(solution)/shard_map/knn_finish/pallas_call | solution.py:346
  150.5 0.0 copy-done
  150.5 0.0 copy-done.2
  150.5 0.2 conditional.1
  150.8 0.0 copy-start.1
  150.8 0.8 copy-done.1
  (2 shorter events, 0.0 us)
Async XLA Ops:
  12.6 137.9 %copy-start = (bf16[32,896]{1,0:T(8,128)(2,1)S(1)}, bf16[32,896]{1,0:T(8,128)(2,1)}, u32[]{:S(2)}) copy-start(bf16[32,896]{1,0:T(8,128)(2,1)} %q_ref.1) | copy-start | bytes 172036
  12.7 137.9 %copy-start.2 = (s32[16384]{0:T(1024)S(1)}, s32[16384]{0:T(1024)}, u32[]{:S(2)}) copy-start(s32[16384]{0:T(1024)} %param.11) | copy-start | bytes 196612
  150.8 0.8 copy-start.1

commit v2 on v1

--- a/solution.py
+++ b/solution.py
@@ -10,28 +10,26 @@
 MESH = pl.DeviceIdType.MESH
 LANES = 128
 BLK = 1024
-SUB = 256
+SUB = 512
 F32 = jnp.float32
 
 
-def _bit_reverse(k, bits):
-    out = 0
-    for i in range(bits):
-        out |= ((k >> i) & 1) << (bits - 1 - i)
-    return out
+DUP = 1 << 16
+TILE_ROWS = 16
 
 
 def _exchange_kernel(
-    cfg, start_ref, inv_ref, tau_ref, q4_ref, q_ref, tok_ref, keys_hbm, w_hbm,
+    cfg, tau_ref, q_ref, sorted_ref, inv_hbm, keys_hbm, w_hbm,
     recv_ref, stats_out, logits_ref,
-    kbuf, scores, wbuf, send, stats, stats_recv,
+    q4_ref, tok_ref, inv_ref, isem, start_vmem, start_ref, stsem, kbuf, scores, wbuf, send, stats, stats_recv,
     ksem, wsem, lsem, send_sem, recv_sem, ssend_sem, srecv_sem, osem,
 ):
-    group, rows, cap, cols, copies, vrows = cfg
+    group, rows, cap, cols, copies, vrows, side = cfg
     me = lax.axis_index("model")
     n_local = keys_hbm.shape[0]
     nblk = n_local // BLK
     crows = cap // copies
+    tile = TILE_ROWS * copies
     qrows = q_ref.shape[0]
 
     barrier = pltpu.get_barrier_semaphore()
@@ -47,7 +45,34 @@
     key_copy(0, 0).start()
     key_copy(1, 1).start()
     w_copy = pltpu.make_async_copy(w_hbm, wbuf, wsem)
+    inv_copy = pltpu.make_async_copy(inv_hbm, inv_ref.at[pl.ds(0, n_local)], isem)
+    inv_copy.start()
+    for i in range(tile):
+        inv_ref[n_local + i] = 0
     tau = tau_ref[0]
+
+    qt = jnp.concatenate([q_ref[...].astype(F32)] * copies, axis=0)
+    for j in range(qt.shape[1] // LANES):
+        q4_ref[j * LANES:(j + 1) * LANES, :] = qt[:, j * LANES:(j + 1) * LANES].T.astype(jnp.bfloat16)
+    krows = sorted_ref.shape[0]
+    tok_ref[:krows, :] = sorted_ref[...]
+    tok_ref[krows:, :] = jnp.zeros((tok_ref.shape[0] - krows, LANES), jnp.int32)
+    start_vmem[...] = jnp.zeros(start_vmem.shape, jnp.int32)
+    for d in range(group + 1):
+        below = jnp.where(sorted_ref[...] < d * cols, 1, 0).reshape(krows // 8, 8, LANES)
+        part = below[0]
+        for i in range(1, krows // 8):
+            part = part + below[i]
+        for i in (4, 2, 1):
+            part = part[:i] + part[i:2 * i]
+        start_vmem[d:d + 1, :] = part
+    counts = start_vmem[...]
+    turn = LANES // 2
+    while turn:
+        counts = counts + pltpu.roll(counts, turn, axis=1)
+        turn //= 2
+    start_vmem[...] = counts
+    start_copy = pltpu.make_async_copy(start_vmem, start_ref, stsem)
 
     def block(b, best):
         slot = lax.rem(b, 3)
@@ -55,6 +80,10 @@
         @pl.when(b + 2 < nblk)
         def _():
             key_copy(b + 2, lax.rem(b + 2, 3)).start()
+
+        @pl.when(b == 1)
+        def _():
+            start_copy.start()
 
         key_copy(b, slot).wait()
 
@@ -76,6 +105,8 @@
     w_copy.start()
     row_max = jnp.max(best, axis=0, keepdims=True)
 
+    inv_copy.wait()
+    start_copy.wait()
     pl.semaphore_wait(barrier, group - 1)
 
     lane_group = lax.broadcasted_iota(jnp.int32, (1, LANES), 1) // qrows
@@ -92,28 +123,33 @@
             device_id={"model": dest}, device_id_type=MESH,
         )
 
-    bits = group.bit_length() - 1
-
-    def offset_of(j):
-        k = 0
-        for i in range(bits):
-            k = k + lax.rem(lax.div(j, 1 << i), 2) * (1 << (bits - 1 - i))
-        return k
-
-    def pack(k, total):
-        dest = lax.rem(me + k, group)
-        first = start_ref[dest]
-        count = start_ref[dest + 1] - first
-
-        @pl.loop(0, crows // 8)
+    def far_first(i, n):
+        odd = lax.rem(i, 2)
+        return n // 2 + (1 - odd) * lax.div(i, 2) - odd * lax.div(i + 1, 2)
+
+    def dest_of(j):
+        if side == 0:
+            return lax.rem(me + 1 + j, group)
+        y, x, c = lax.div(me, 2 * side), lax.rem(lax.div(me, 2), side), lax.rem(me, 2)
+        dy = far_first(lax.rem(j, side), side)
+        dx = far_first(lax.div(j, 2 * side), side)
+        dc = 1 - lax.rem(lax.div(j, side), 2)
+        return (lax.rem(y + dy, side) * side + lax.rem(x + dx, side)) * 2 + lax.rem(c + dc, 2)
+
+    def pack(k, dest, total):
+        first = jnp.clip(start_ref[dest, 0], 0, n_local)
+        count = start_ref[dest + 1, 0] - first
+
+        @pl.loop(0, crows // TILE_ROWS)
         def _(t):
-            base = first + t * (8 * copies)
-            for r in range(8):
-                parts = [scores[pl.ds(inv_ref[base + r * copies + g], 1), :] for g in range(copies)]
+            base = jnp.minimum(first + t * tile, n_local)
+            near = [inv_ref.at[pl.ds(i, n_local + 1)][base] for i in range(tile)]
+            for r in range(TILE_ROWS):
+                parts = [scores[pl.ds(near[r * copies + g], 1), :] for g in range(copies)]
                 row = parts[copies - 1]
                 for g in range(copies - 2, -1, -1):
                     row = jnp.where(lane_group == g, parts[g], row)
-                send[k, pl.ds(t * 8 + r, 1), :] = row
+                send[k, pl.ds(t * TILE_ROWS + r, 1), :] = row
 
         w = jnp.where(entry < count, jnp.exp(send[k, :crows, :] - row_max), 0.0)
         send[k, :crows, :] = w
@@ -122,19 +158,20 @@
         low = pltpu.roll(tok_ref[pl.ds(at, 8), :], LANES - shift, axis=1)
         high = pltpu.roll(tok_ref[pl.ds(at + 1, 8), :], LANES - shift, axis=1)
         tok = jnp.where(id_lane < LANES - shift, low, high) - dest * cols
-        send[k, crows:crows + 8, :] = jnp.where(id_pos < count, tok, cols).astype(F32)
+        tok = jnp.where(id_pos < count, tok, cols + lax.rem(lax.div(id_pos, copies), TILE_ROWS))
+        send[k, crows:crows + 8, :] = jnp.where(id_pos < 7 * LANES, tok, count).astype(F32)
         return total + jnp.sum(w.reshape(crows // 8, 8, LANES), axis=0)
 
     def step(j, total):
-        k = offset_of(j)
-        total = pack(k, total)
-        block_send(k, lax.rem(me + k, group)).start()
+        total = pack(j, dest_of(j), total)
+        block_send(j - 1, dest_of(j - 1)).start()
         return total
 
-    total = lax.fori_loop(1, group, step, jnp.zeros((8, LANES), F32))
-    total = pack(0, total)
-    own = pltpu.make_async_copy(send.at[0], recv_ref.at[me], lsem)
-    own.start()
+    total = pack(0, dest_of(0), jnp.zeros((8, LANES), F32))
+    total = lax.fori_loop(1, group - 1, step, total)
+    total = pack(group - 1, me, total)
+    block_send(group - 2, dest_of(group - 2)).start()
+    own = pltpu.make_async_copy(send.at[group - 1], recv_ref.at[me], lsem)
 
     w_copy.wait()
     def head(at, size, carry):
@@ -151,7 +188,7 @@
     lm_max_row, lm_sum_row = carry
 
     def worst(d, c):
-        return jnp.maximum(c, start_ref[d + 1] - start_ref[d])
+        return jnp.maximum(c, start_ref[d + 1, 0] - start_ref[d, 0])
 
     most = lax.fori_loop(0, group, worst, jnp.int32(0))
     over = jnp.where(most > cap, 1.0, 0.0).astype(F32)
@@ -161,6 +198,8 @@
     stats[3:4, :] = lm_sum_row
     stats[4:5, :] = jnp.full((1, LANES), over, F32)
     stats[5:8, :] = jnp.zeros((3, LANES), F32)
+    own.start()
+    own.wait()
 
     def stat_send(k, dest):
         return pltpu.make_async_remote_copy(
@@ -182,28 +221,42 @@
             device_id={"model": src}, device_id_type=MESH,
         ).wait_recv()
         pltpu.make_async_remote_copy(
-            src_ref=send.at[k], dst_ref=recv_ref.at[src], send_sem=send_sem.at[k], recv_sem=recv_sem.at[src],
+            src_ref=send.at[k - 1], dst_ref=recv_ref.at[src], send_sem=send_sem.at[k - 1], recv_sem=recv_sem.at[src],
             device_id={"model": src}, device_id_type=MESH,
         ).wait_recv()
 
     @pl.loop(1, group)
     def _(k):
-        block_send(k, lax.rem(me + k, group)).wait_send()
+        block_send(k - 1, dest_of(k - 1)).wait_send()
         stat_send(k, lax.rem(me + k, group)).wait_send()
 
-    own.wait()
     stats_out[...] = stats_recv[...]
 
 
 def _finish_kernel(
-    cfg, mix_ref, stats_ref, recv_ref, logits_ref, out_ref, hist0, hist1, hist2, hist3, scaled, idbuf, ids, sem
+    cfg, mix_ref, stats_ref, recv_ref, logits_hbm, out_ref, over_ref,
+    hist0, hist1, hist2, hist3, scaled, logits_ref, idbuf, ids, sem, lsem,
 ):
-    group, rows, cap, cols, copies, vrows = cfg
+    group, rows, cap, cols, copies, vrows, side = cfg
     crows = cap // copies
     hists = (hist0, hist1, hist2, hist3)
-    idbuf[...] = recv_ref[:, crows:crows + 8, :].astype(jnp.int32)
+    logits_copy = pltpu.make_async_copy(logits_hbm, logits_ref, lsem)
+    logits_copy.start()
+    tile = TILE_ROWS * copies
+    lane3 = lax.broadcasted_iota(jnp.int32, (8, LANES), 1)
+    row3 = lax.broadcasted_iota(jnp.int32, (8, LANES), 0)
+    for s in range(group):
+        v = recv_ref[s, crows:crows + 8, :].astype(jnp.int32)
+        same = (v == pltpu.roll(v, LANES - copies, axis=1)) & (lax.rem(lane3, tile) < tile - copies)
+        flag = jnp.where(same, 1, 0)
+        step = tile // 2
+        while step:
+            flag = flag | pltpu.roll(flag, LANES - step, axis=1)
+            step //= 2
+        count = jnp.sum(jnp.where((lane3 == 0) & (row3 == 7), v, 0).astype(F32)).astype(jnp.int32)
+        flag = jnp.where(row3 * LANES + lane3 < count, flag, 2)
+        idbuf[s] = v + jnp.where((lax.rem(lane3, tile) == 0) & (row3 < 7), flag * DUP, 0)
     id_copy = pltpu.make_async_copy(idbuf, ids, sem)
-    id_copy.start()
 
     st = stats_ref[...]
     m_all = st[:, 0, :]
@@ -214,59 +267,73 @@
     lm = jnp.max(lm_all, axis=0, keepdims=True)
     lmz = jnp.sum(st[:, 3, :] * jnp.exp(lm_all - lm), axis=0, keepdims=True)
 
-    @pl.loop(0, vrows // 8)
+    @pl.loop(0, vrows // 32)
     def _(i):
         for h in hists:
-            h[pl.ds(i * 8, 8), :] = jnp.zeros((8, LANES), F32)
-
+            h[pl.ds(i * 32, 32), :] = jnp.zeros((32, LANES), F32)
+
+    id_copy.start()
     for s in range(group):
         scaled[s] = recv_ref[s, :crows, :] * scale[s:s + 1, :]
     id_copy.wait()
 
+    per = LANES // tile
+
+    def tile_add(s, near, t, k):
+        code = near[k * tile]
+        at = lambda i: near[k * tile + i] if i else code & (DUP - 1)
+
+        @pl.when(code < DUP)
+        def _():
+            rows_ = [scaled[s, pl.ds(t * TILE_ROWS + r, 1), :] for r in range(TILE_ROWS)]
+            for g in range(copies):
+                at_g = [at(r * copies + g) for r in range(TILE_ROWS)]
+                new = [hists[g][pl.ds(v, 1), :] + row for v, row in zip(at_g, rows_)]
+                for v, x in zip(at_g, new):
+                    hists[g][pl.ds(v, 1), :] = x
+
+        @pl.when((code >= DUP) & (code < 2 * DUP))
+        def _():
+            for r in range(TILE_ROWS):
+                row = scaled[s, pl.ds(t * TILE_ROWS + r, 1), :]
+                for g in range(copies):
+                    v = at(r * copies + g)
+                    hists[g][pl.ds(v, 1), :] = hists[g][pl.ds(v, 1), :] + row
+
     @pl.loop(0, group)
     def _(s):
-        @pl.loop(0, crows // 8)
-        def _(t):
-            sub = lax.div(t, LANES // (8 * copies))
-            lane0 = lax.rem(t, LANES // (8 * copies)) * (8 * copies)
-            for r in range(8):
-                row = scaled[s, pl.ds(t * 8 + r, 1), :]
-                for g in range(copies):
-                    v = ids[s, sub, lane0 + r * copies + g]
-                    hists[g][pl.ds(v, 1), :] = hists[g][pl.ds(v, 1), :] + row
+        @pl.loop(0, lax.div(jnp.minimum(ids[s, 7, 0], cap) + (LANES - 1), LANES))
+        def _(sub):
+            near = [ids.at[:, :, pl.ds(i, 1)][s, sub, 0] for i in range(LANES)]
+            for k in range(per):
+                tile_add(s, near, sub * per + k, k)
+
+    over_ref[0] = jnp.max(st[:, 4, :]).astype(jnp.int32)
+    logits_copy.wait()
 
     qrows = out_ref.shape[0]
     lane = lax.broadcasted_iota(jnp.int32, (LANES, LANES), 1)
-    eye = lane == lax.broadcasted_iota(jnp.int32, (LANES, LANES), 0)
-
-    def column(row):
-        return jnp.sum(jnp.where(eye, row, 0.0), axis=1, keepdims=True)
-
-    zc = column(z)
-    z_col = zc[:qrows]
+    z8 = jnp.broadcast_to(z, (8, LANES))
+    z_all = z8
     for g in range(1, copies):
-        z_col = z_col + zc[g * qrows:(g + 1) * qrows]
-    lmz_col = column(lmz)[:qrows]
+        z_all = z_all + pltpu.roll(z8, g * qrows, axis=1)
     mix = mix_ref[0]
-    a = mix / z_col
-    b = (1.0 - mix) / lmz_col
+    a = mix / z_all[0:1]
+    b = jnp.where(lane[0:1] < qrows, (1.0 - mix) / lmz, 0.0)
     for c in range(pl.cdiv(cols, LANES)):
         width = min(LANES, cols - c * LANES)
-        hrows = min(LANES, vrows - c * LANES)
-        acc = hists[0][c * LANES:c * LANES + hrows, :]
+        part = slice(c * LANES, c * LANES + width)
+        acc = hists[0][part, :]
         for g in range(1, copies):
-            acc = jnp.where(lane[:hrows] // qrows >= g, hists[g][c * LANES:c * LANES + hrows, :], acc)
-        if hrows < LANES:
-            acc = jnp.concatenate([acc, jnp.zeros((LANES - hrows, LANES), F32)], axis=0)
-        tr = acc.T
-        h = tr[:qrows]
+            acc = jnp.where(lane[:width] >= g * qrows, hists[g][part, :], acc)
+        x = acc * a + jnp.exp(logits_ref[part, :] - lm) * b
+        if width < LANES:
+            x = jnp.concatenate([x, jnp.zeros((LANES - width, LANES), F32)], axis=0)
+        tr = x.T
+        p = tr[:qrows]
         for g in range(1, copies):
-            h = h + tr[g * qrows:(g + 1) * qrows]
-        e = jnp.exp(logits_ref[c * LANES:c * LANES + width, :] - lm)
-        if width < LANES:
-            e = jnp.concatenate([e, jnp.zeros((LANES - width, LANES), F32)], axis=0)
-        e = e.T[:qrows, :width]
-        out_ref[:, c * LANES:c * LANES + width] = jnp.log(h[:, :width] * a + e * b)
+            p = p + tr[g * qrows:(g + 1) * qrows]
+        out_ref[:, part] = jnp.log(p[:, :width])
 
 
 def solution(mesh):
@@ -297,17 +364,15 @@
         cols = w_shard.shape[1]
         copies = LANES // rows
         mean = n_local // group
-        cap = -(-int(mean + 5.6 * mean ** 0.5) // 32) * 32
+        cap = -(-int(mean + 5.6 * mean ** 0.5) // (TILE_ROWS * copies)) * (TILE_ROWS * copies)
         crows = cap // copies
-        vrows = (cols // 8 + 1) * 8
-        cfg = (group, rows, cap, cols, copies, vrows)
-
+        vrows = -(-(cols + TILE_ROWS) // 32) * 32
+        side = int((group // 2) ** 0.5)
+        side = side if side * side * 2 == group and side in (2, 4) else 0
+        cfg = (group, rows, cap, cols, copies, vrows, side)
+        srows = -(-(group + 1) // 8) * 8
+        assert n_local % (8 * LANES) == 0 and cap <= 7 * LANES and vrows < DUP
         tok_sorted, inv = lax.sort((tok_shard, lax.iota(jnp.int32, n_local)), num_keys=1)
-        bounds = lax.iota(jnp.int32, group + 1) * cols
-        start = jnp.sum((tok_sorted[None, :] < bounds[:, None]).astype(jnp.int32), axis=1)
-        inv = jnp.pad(inv, (0, cap))
-        tok2d = jnp.pad(tok_sorted, (0, 16 * LANES)).reshape(n_local // LANES + 16, LANES)
-        q4 = jnp.tile(queries.T, (1, copies))
 
         smem = pl.BlockSpec(memory_space=pltpu.SMEM)
         vmem = pl.BlockSpec(memory_space=pltpu.VMEM)
@@ -319,9 +384,16 @@
                 jax.ShapeDtypeStruct((group, 8, LANES), F32),
                 jax.ShapeDtypeStruct((cols, LANES), F32),
             ),
-            in_specs=[smem, smem, smem, vmem, vmem, vmem, hbm, hbm],
+            in_specs=[smem, vmem, vmem, hbm, hbm, hbm],
             out_specs=(hbm, vmem, vmem),
             scratch_shapes=[
+                pltpu.VMEM((dim, LANES), jnp.bfloat16),
+                pltpu.VMEM((n_local // LANES + 16, LANES), jnp.int32),
+                pltpu.SMEM((n_local + TILE_ROWS * copies,), jnp.int32),
+                pltpu.SemaphoreType.DMA,
+                pltpu.VMEM((srows, LANES), jnp.int32),
+                pltpu.SMEM((srows, LANES), jnp.int32),
+                pltpu.SemaphoreType.DMA,
                 pltpu.VMEM((3, BLK, dim), jnp.bfloat16),
                 pltpu.VMEM((n_local, LANES), F32),
                 pltpu.VMEM((cols, dim), jnp.bfloat16),
@@ -341,27 +413,28 @@
                 collective_id=0, has_side_effects=True, vmem_limit_bytes=60 * 1024 * 1024
             ),
             name="knn_exchange",
-        )(start, inv, temperature, q4, queries, tok2d, key_shard, w_shard.T)
-
-        fast = pl.pallas_call(
+        )(temperature, queries, tok_sorted.reshape(n_local // LANES, LANES), inv, key_shard, w_shard.T)
+
+        fast, over = pl.pallas_call(
             functools.partial(_finish_kernel, cfg),
-            out_shape=jax.ShapeDtypeStruct((rows, cols), F32),
-            in_specs=[smem, vmem, vmem, vmem],
-            out_specs=vmem,
+            out_shape=(jax.ShapeDtypeStruct((rows, cols), F32), jax.ShapeDtypeStruct((1,), jnp.int32)),
+            in_specs=[smem, vmem, vmem, hbm],
+            out_specs=(vmem, smem),
             scratch_shapes=[pltpu.VMEM((vrows, LANES), F32)] * 4
             + [
                 pltpu.VMEM((group, crows, LANES), F32),
+                pltpu.VMEM((cols, LANES), F32),
                 pltpu.VMEM((group, 8, LANES), jnp.int32),
                 pltpu.SMEM((group, 8, LANES), jnp.int32),
+                pltpu.SemaphoreType.DMA,
                 pltpu.SemaphoreType.DMA,
             ],
             compiler_params=pltpu.CompilerParams(vmem_limit_bytes=60 * 1024 * 1024),
             name="knn_finish",
         )(mix_weight, stats, recv, logits)
 
-        overflow = jnp.max(stats[:, 4, 0]) > 0.0
         args = (queries, w_shard, key_shard, tok_shard, temperature, mix_weight)
-        return lax.cond(overflow, lambda: dense_path(*args), lambda: fast)
+        return lax.cond(over[0] > 0, lambda: dense_path(*args), lambda: fast)
 
     return jax.shard_map(
         local_step,

time: 152 us -> 110 us (0.72)
  Pallas kernels: 135 us -> 98.4 us
  local copies, waits for them, and re-layouts: 3.78 us -> 0.84 us
  other arithmetic: 10.6 us -> 8.62 us
    pallas_call x1, Pallas kernels: 62.6 us -> 33 us  [local_step(): pl.pallas_call(functools.partial(_finish_kernel, cfg), out_shape=(jax.Sha...]
    pallas_call x1, Pallas kernels: 72.4 us -> 65.4 us  [local_step(): pl.pallas_call(functools.partial(_exchange_kernel, cfg), out_shape=(jax.S...]
    another operation x2 -> x0, local copies, waits for them, and re-layouts: 1.67 us -> none  [local_step(): q4 = jnp.tile(queries.T, (1, copies))]
    reduce_max x1 -> x0, other arithmetic: 1.54 us -> none  [local_step(): overflow = jnp.max(stats[:, 4, 0]) > 0.0]
where the time goes in v2:
time: 110 us
  Pallas kernels  98.4 us (89%)
  other arithmetic  8.62 us (8%)
  between operations  2.01 us (2%)
    pallas_call x1, Pallas kernels, local_step(): pl.pallas_call(functools.partial(_exchange_kernel, cfg), out_shape=(jax.S...  65.4 us
    pallas_call x1, Pallas kernels, local_step(): pl.pallas_call(functools.partial(_finish_kernel, cfg), out_shape=(jax.Sha...  33 us
    sort x1, other arithmetic, local_step(): lax.sort((tok_shard, lax.iota(jnp.int32, n_local)), num_keys=1)  8.62 us

profile of v2, /device:TPU:97, one launch (start us, length us, event | category | flops | bytes accessed | tf_op | source)
XLA Modules:
  0.0 110.1 jit_solution(11122818970080255388)
XLA Ops:
  1.3 8.6 %sort.15 = (s32[16384]{0:T(1024)}, s32[16384]{0:T(1024)}) sort(s32[16384]{0:T(1024)} %param.11, s32[16384]{0:T(1024)S(1)} %iota.3), dimensions={0}, to_apply=%region_0.0 | sort | flops 229376 | bytes 262144 | tf_op jit(solution)/shard_map/sort | solution.py:375
  9.9 0.0 copy-start
  9.9 0.0 copy-start.1
  9.9 65.4 %knn_exchange.1 = (f32[32,168,128]{2,1,0:T(8,128)}, f32[32,8,128]{2,1,0:T(8,128)}, f32[4748,128]{1,0:T(8,128)}) custom-call(f32[1]{0:T(128)S(6)} %copy.21.tau_ref, bf16[32,896]{1,0:T(8,128)(2,1)} %q_ref.1, s32[128,128]{1,0:T(8,128)} %bitcast.14, s32[16384]{0:T(1024)} %get-tuple-element.35.inv_hbm, bf16[16384,896]{1,0:T(8,128)(2,1)} %keys_hbm.1, ...), custom_call_target="tpu_custom_call" | custom-call | tf_op jit(solution)/shard_map/knn_exchange/pallas_call | solution.py:380
  75.4 33.0 %knn_finish.1 = (f32[32,4748]{1,0:T(8,128)S(1)}, s32[1]{0:T(128)}) custom-call(f32[1]{0:T(128)S(6)} %copy.22.mix_ref, f32[32,8,128]{2,1,0:T(8,128)} %get-tuple-element.36.stats_ref, f32[32,168,128]{2,1,0:T(8,128)} %get-tuple-element.37.recv_ref, f32[4748,128]{1,0:T(8,128)} %get-tuple-element.38.logits_hbm), custom_call_target="tpu_custom_call" | custom-call | tf_op jit(solution)/shard_map/knn_finish/pallas_call | solution.py:418
  109.0 0.0 copy-done
  109.0 0.0 copy-done.1
  109.0 0.2 conditional.1
  109.3 0.0 copy-start.2
  109.3 0.8 copy-done.2
  (1 shorter events, 0.0 us)
Async XLA Ops:
  9.9 99.1 %copy-start = (bf16[32,896]{1,0:T(8,128)(2,1)S(1)}, bf16[32,896]{1,0:T(8,128)(2,1)}, u32[]{:S(2)}) copy-start(bf16[32,896]{1,0:T(8,128)(2,1)} %q_ref.1) | copy-start | bytes 172036
  9.9 99.1 %copy-start.1 = (s32[16384]{0:T(1024)S(1)}, s32[16384]{0:T(1024)}, u32[]{:S(2)}) copy-start(s32[16384]{0:T(1024)} %param.11) | copy-start | bytes 196612
  109.3 0.8 copy-start.2

commit v3 on v2

--- a/solution.py
+++ b/solution.py
@@ -132,7 +132,7 @@
             return lax.rem(me + 1 + j, group)
         y, x, c = lax.div(me, 2 * side), lax.rem(lax.div(me, 2), side), lax.rem(me, 2)
         dy = far_first(lax.rem(j, side), side)
-        dx = far_first(lax.div(j, 2 * side), side)
+        dx = far_first(lax.rem(lax.div(j, 2 * side) + lax.rem(j, side) + 1, side), side)
         dc = 1 - lax.rem(lax.div(j, side), 2)
         return (lax.rem(y + dy, side) * side + lax.rem(x + dx, side)) * 2 + lax.rem(c + dc, 2)
 

time: 110 us -> 107 us (0.973)
  Pallas kernels: 98.4 us -> 95.5 us
    pallas_call x1, Pallas kernels: 65.4 us -> 62.4 us  [local_step(): pl.pallas_call(functools.partial(_exchange_kernel, cfg), out_shape=(jax.S...]
where the time goes in v3:
time: 107 us
  Pallas kernels  95.5 us (89%)
  other arithmetic  8.62 us (8%)
  between operations  2.01 us (2%)
    pallas_call x1, Pallas kernels, local_step(): pl.pallas_call(functools.partial(_exchange_kernel, cfg), out_shape=(jax.S...  62.4 us
    pallas_call x1, Pallas kernels, local_step(): pl.pallas_call(functools.partial(_finish_kernel, cfg), out_shape=(jax.Sha...  33.1 us
    sort x1, other arithmetic, local_step(): lax.sort((tok_shard, lax.iota(jnp.int32, n_local)), num_keys=1)  8.62 us

profile of v3, /device:TPU:97, one launch (start us, length us, event | category | flops | bytes accessed | tf_op | source)
XLA Modules:
  0.0 107.2 jit_solution(2932101463624263033)
XLA Ops:
  1.3 8.6 %sort.15 = (s32[16384]{0:T(1024)}, s32[16384]{0:T(1024)}) sort(s32[16384]{0:T(1024)} %param.11, s32[16384]{0:T(1024)S(1)} %iota.3), dimensions={0}, to_apply=%region_0.0 | sort | flops 229376 | bytes 262144 | tf_op jit(solution)/shard_map/sort | solution.py:375
  9.9 0.0 copy-start
  9.9 0.0 copy-start.1
  9.9 62.4 %knn_exchange.1 = (f32[32,168,128]{2,1,0:T(8,128)}, f32[32,8,128]{2,1,0:T(8,128)}, f32[4748,128]{1,0:T(8,128)}) custom-call(f32[1]{0:T(128)S(6)} %copy.21.tau_ref, bf16[32,896]{1,0:T(8,128)(2,1)} %q_ref.1, s32[128,128]{1,0:T(8,128)} %bitcast.14, s32[16384]{0:T(1024)} %get-tuple-element.35.inv_hbm, bf16[16384,896]{1,0:T(8,128)(2,1)} %keys_hbm.1, ...), custom_call_target="tpu_custom_call" | custom-call | tf_op jit(solution)/shard_map/knn_exchange/pallas_call | solution.py:380
  72.3 33.1 %knn_finish.1 = (f32[32,4748]{1,0:T(8,128)S(1)}, s32[1]{0:T(128)}) custom-call(f32[1]{0:T(128)S(6)} %copy.22.mix_ref, f32[32,8,128]{2,1,0:T(8,128)} %get-tuple-element.36.stats_ref, f32[32,168,128]{2,1,0:T(8,128)} %get-tuple-element.37.recv_ref, f32[4748,128]{1,0:T(8,128)} %get-tuple-element.38.logits_hbm), custom_call_target="tpu_custom_call" | custom-call | tf_op jit(solution)/shard_map/knn_finish/pallas_call | solution.py:418
  106.1 0.0 copy-done
  106.1 0.0 copy-done.1
  106.1 0.2 conditional.1
  106.3 0.0 copy-start.2
  106.3 0.8 copy-done.2
  (1 shorter events, 0.0 us)
Async XLA Ops:
  9.9 96.1 %copy-start = (bf16[32,896]{1,0:T(8,128)(2,1)S(1)}, bf16[32,896]{1,0:T(8,128)(2,1)}, u32[]{:S(2)}) copy-start(bf16[32,896]{1,0:T(8,128)(2,1)} %q_ref.1) | copy-start | bytes 172036
  9.9 96.2 %copy-start.1 = (s32[16384]{0:T(1024)S(1)}, s32[16384]{0:T(1024)}, u32[]{:S(2)}) copy-start(s32[16384]{0:T(1024)} %param.11) | copy-start | bytes 196612
  106.3 0.8 copy-start.2
